TPU v7x, 32 devices: a whole 2x2x4 slice. The times are simulated.
32 devices in a mesh: dp: 16 (over z, x, core), seq: 2 (over y).
Axes of the slice: x: 2, y: 2, z: 4, core: 2. Of those that a mesh axis runs over, the one named last changes fastest.
Arguments:
- queries: bfloat16 [4096, 6144], P(('dp', 'seq')), may hold values from -8 to 8
- latent: bfloat16 [4096, 512], P(('dp', 'seq')), may hold values from -6 to 6
- key_rope: bfloat16 [4096, 64], P(('dp', 'seq')), may hold values from -8 to 8
- up_weight: bfloat16 [512, 8192], P(None, 'seq'), may hold values from -0.25 to 0.25
- out_grad: bfloat16 [4096, 4096], P(('dp', 'seq')), may hold values from -6 to 6
Outputs:
- latent_grad: float32 [4096, 512], P(('dp', 'seq'))
- weight_grad: float32 [512, 8192], P('dp', 'seq')
All inputs are finite; a program needn't handle non-finite values.
Results may differ from a plain program's by a relative error of at most 0.0065.
Values may be sent and summed in bfloat16 or wider, within the bound.
A program may use at most 64 MiB of HBM per device.

v0:
```python
import math

import jax
import jax.numpy as jnp
from jax import lax
from jax.sharding import PartitionSpec as P

NOPE = 128
ROPE = 64
VDIM = 128


def per_device(queries, latent, key_rope, up_weight, out_grad):
    query_width = NOPE + ROPE
    kv_width = NOPE + VDIM
    score_scale = query_width ** (-0.5)
    latent_full, rope_full = (
        lax.all_gather(latent, "seq", axis=0, tiled=True),
        lax.all_gather(key_rope, "seq", axis=0, tiled=True),
    )
    length = latent_full.shape[0]
    local_heads = up_weight.shape[1] // kv_width
    kv_cols = jnp.dot(latent_full, up_weight, preferred_element_type=jnp.float32).astype(
        jnp.bfloat16
    )
    block_rows = math.gcd(length, 512)

    def head_block(head_index, query_all, grad_out):
        kv_all = lax.dynamic_slice_in_dim(kv_cols, head_index * kv_width, kv_width, 1)
        query_nope = query_all[:, :NOPE]
        query_rope = query_all[:, NOPE:]
        keys_nope = kv_all[:, :NOPE]
        values = kv_all[:, NOPE:]
        key_grad = jnp.zeros((length, NOPE), jnp.float32)
        value_grad = jnp.zeros((length, VDIM), jnp.float32)
        for segment in range(length // block_rows):
            row_start = segment * block_rows
            row_end = row_start + block_rows
            scores = jnp.dot(
                query_nope[row_start:row_end],
                keys_nope[:row_end].T,
                preferred_element_type=jnp.float32,
            )
            scores = scores + jnp.dot(
                query_rope[row_start:row_end],
                rope_full[:row_end].T,
                preferred_element_type=jnp.float32,
            )
            scores = scores * score_scale
            query_pos = row_start + lax.broadcasted_iota(jnp.int32, (block_rows, row_end), 0)
            key_pos = lax.broadcasted_iota(jnp.int32, (block_rows, row_end), 1)
            scores = jnp.where(key_pos <= query_pos, scores, jnp.float32(-1e30))
            row_max = jnp.max(scores, axis=1, keepdims=True)
            expo = jnp.exp(scores - row_max)
            attend = expo / jnp.sum(expo, axis=1, keepdims=True)
            attend_rounded = attend.astype(jnp.bfloat16)
            grad_rows = grad_out[row_start:row_end]
            value_grad = value_grad.at[:row_end].add(
                jnp.dot(attend_rounded.T, grad_rows, preferred_element_type=jnp.float32)
            )
            prob_grad = jnp.dot(grad_rows, values[:row_end].T, preferred_element_type=jnp.float32)
            row_dot = jnp.sum(attend * prob_grad, axis=1, keepdims=True)
            score_grad = (attend * (prob_grad - row_dot) * score_scale).astype(jnp.bfloat16)
            key_grad = key_grad.at[:row_end].add(
                jnp.dot(
                    score_grad.T, query_nope[row_start:row_end], preferred_element_type=jnp.float32
                )
            )
        return jnp.concatenate([key_grad, value_grad], axis=1).astype(jnp.bfloat16)

    start_cols = jnp.zeros((length, local_heads * kv_width), jnp.bfloat16)
    query_heads, grad_heads = (
        lax.all_to_all(queries, "seq", split_axis=1, concat_axis=0, tiled=True),
        lax.all_to_all(out_grad, "seq", split_axis=1, concat_axis=0, tiled=True),
    )

    def one_head(head_index, grad_cols):
        query_all = lax.dynamic_slice_in_dim(query_heads, head_index * query_width, query_width, 1)
        grad_out = lax.dynamic_slice_in_dim(grad_heads, head_index * VDIM, VDIM, 1)
        joined = head_block(head_index, query_all, grad_out)
        return lax.dynamic_update_slice_in_dim(grad_cols, joined, head_index * kv_width, 1)

    grad_cols = lax.fori_loop(0, local_heads, one_head, start_cols)
    latent_part = jnp.dot(grad_cols, up_weight.T, preferred_element_type=jnp.float32)
    latent_grad = lax.psum_scatter(latent_part, "seq", scatter_dimension=0, tiled=True)
    replicas = lax.axis_size("dp")
    weight_full = jnp.dot(latent_full.T, grad_cols, preferred_element_type=jnp.float32)
    summed = lax.psum_scatter(weight_full, "dp", scatter_dimension=0, tiled=True)
    return (latent_grad, summed / replicas)


def solution(mesh):
    placed = (
        P(("dp", "seq"), None),
        P(("dp", "seq"), None),
        P(("dp", "seq"), None),
        P(None, "seq"),
        P(("dp", "seq"), None),
    )
    return jax.shard_map(
        per_device,
        mesh=mesh,
        in_specs=placed,
        out_specs=(P(("dp", "seq"), None), P("dp", "seq")),
        check_vma=False,
    )
```

profile of v0, /device:TPU:0, one launch (start us, length us, event | category | flops | bytes accessed | tf_op | source)
XLA Modules:
  0.0 284.1 jit_solution(16599826877233286774)
XLA Ops:
  7.2 2.4 copy.22
  9.6 4.3 %all-to-all-start.1 = ((bf16[128,2,2048]{2,0,1:T(8,128)(2,1)}), bf16[128,2,2048]{2,0,1:T(8,128)(2,1)S(1)}, u32[]{:S(2)}, u32[]{:S(2)}) async-start(bf16[128,2,2048]{2,0,1:T(8,128)(2,1)} %bitcast.23), calls=%async_computation.1 | async-start | bytes 2097152 | tf_op jit(solution)/shard_map/all_to_all | solution.py:74
  13.9 1.3 copy.21
  15.1 13.2 %all-to-all-done.1 = bf16[128,2,2048]{2,0,1:T(8,128)(2,1)S(1)} async-done(((bf16[128,2,2048]{2,0,1:T(8,128)(2,1)}), bf16[128,2,2048]{2,0,1:T(8,128)(2,1)S(1)}, u32[]{:S(2)}, u32[]{:S(2)}) %all-to-all-start.1) | async-done | bytes 1048608 | tf_op jit(solution)/shard_map/all_to_all | solution.py:74
  28.3 3.7 %all-to-all-start = ((bf16[128,2,3072]{2,0,1:T(8,128)(2,1)}), bf16[128,2,3072]{2,0,1:T(8,128)(2,1)S(1)}, u32[]{:S(2)}, u32[]{:S(2)}) async-start(bf16[128,2,3072]{2,0,1:T(8,128)(2,1)} %bitcast.22), calls=%async_computation | async-start | bytes 3145728 | tf_op jit(solution)/shard_map/all_to_all | solution.py:73
  32.1 19.4 %all_gather.7 = bf16[256,64]{1,0:T(8,128)(2,1)S(1)} all-gather(bf16[128,64]{1,0:T(8,128)(2,1)S(1)} %copy.12), channel_id=1, replica_groups=mesh['dp'=16,'seq'=2] {'seq'}, dimensions={0}, use_global_device_ids=true | all-gather | bytes 49152 | tf_op jit(solution)/shard_map/all_gather | solution.py:19
  51.6 5.6 %all_gather.6 = bf16[256,512]{1,0:T(8,128)(2,1)S(1)} all-gather(bf16[128,512]{1,0:T(8,128)(2,1)S(1)} %copy-done.2), channel_id=1, replica_groups=mesh['dp'=16,'seq'=2] {'seq'}, dimensions={0}, use_global_device_ids=true | all-gather | bytes 393216 | tf_op jit(solution)/shard_map/all_gather | solution.py:18
  57.2 4.8 %convolution_convert_fusion.2 = bf16[256,4096]{1,0:T(8,128)(2,1)} fusion(bf16[256,512]{1,0:T(8,128)(2,1)S(1)} %all_gather.6, bf16[512,4096]{1,0:T(8,128)(2,1)} %param.18), kind=kOutput, calls=%fused_computation.31 | convolution fusion | flops 1074790400 | bytes 6553600 | tf_op jit(solution)/shard_map/dot_general | solution.py:23
  63.3 79.6 %while.25 = (s32[]{:T(128)}, bf16[256,4096]{0,1:T(8,128)(2,1)S(1)}, bf16[256,3072]{1,0:T(8,128)(2,1)}, bf16[256,4096]{1,0:T(8,128)(2,1)}, bf16[256,64]{1,0:T(8,1...) while((s32[]{:T(128)}, bf16[256,4096]{0,1:T(8,128)(2,1)S(1)}, ...), condition=%wide.region_4.0_spmd, body=%wide.region_0.4_spmd.sunk | while | flops 77135120 | bytes 3255639 | solution.py:83
  63.3 1.2 fusion.48
  67.0 1.2 convolution_convert_fusion.6
  68.3 1.2 fusion.48
  72.0 1.2 convolution_convert_fusion.6
  73.3 1.2 fusion.48
  77.0 1.2 convolution_convert_fusion.6
  78.2 1.2 fusion.48
  81.9 1.2 convolution_convert_fusion.6
  83.2 1.2 fusion.48
  86.9 1.2 convolution_convert_fusion.6
  88.2 1.2 fusion.48
  91.9 1.2 convolution_convert_fusion.6
  93.2 1.2 fusion.48
  96.9 1.2 convolution_convert_fusion.6
  98.1 1.2 fusion.48
  101.8 1.2 convolution_convert_fusion.6
  103.1 1.2 fusion.48
  106.8 1.2 convolution_convert_fusion.6
  108.1 1.2 fusion.48
  111.8 1.2 convolution_convert_fusion.6
  113.1 1.2 fusion.48
  116.8 1.2 convolution_convert_fusion.6
  118.0 1.2 fusion.48
  121.7 1.2 convolution_convert_fusion.6
  126.7 1.2 convolution_convert_fusion.6
  128.0 1.2 fusion.48
  131.7 1.2 convolution_convert_fusion.6
  133.0 1.2 fusion.48
  136.7 1.2 convolution_convert_fusion.6
  137.9 1.2 fusion.48
  141.6 1.2 convolution_convert_fusion.6
  142.9 4.5 %convolution_bitcast_fusion = f32[512,4096]{0,1:T(8,128)} fusion(bf16[256,4096]{0,1:T(8,128)(2,1)S(1)} %get-tuple-element.175, bf16[256,512]{1,0:T(8,128)(2,1)S(1)} %all_gather.6), kind=kOutput, calls=%fused_computation.30 | convolution fusion | flops 1073741824 | bytes 10747904 | tf_op jit(solution)/shard_map/dot_general | solution.py:87
  147.4 9.0 %copy.15 = f32[512,4096]{1,0:T(8,128)} copy(f32[512,4096]{0,1:T(8,128)} %convolution_bitcast_fusion) | data formatting | bytes 16777216
  156.4 4.3 %fusion.25 = f32[256,512]{1,0:T(8,128)} fusion(bf16[256,4096]{0,1:T(8,128)(2,1)S(1)} %get-tuple-element.175, bf16[512,4096]{1,0:T(8,128)(2,1)} %param.18), kind=kOutput, calls=%fused_computation.36 | convolution fusion | flops 1073741824 | bytes 6815744 | tf_op jit(solution)/shard_map/dot_general | solution.py:84
  160.8 99.4 %reduce-scatter.7.cloned.1.call-done = f32[32,4096]{1,0:T(8,128)} async-done(((f32[512,4096]{1,0:T(8,128)}), f32[32,4096]{1,0:T(8,128)}) %reduce-scatter.7.cloned.1.call-update) | async-done | bytes 524304
  260.2 1.6 copy.16
  261.9 1.5 broadcast_multiply_fusion
  263.3 3.0 %copy.14 = f32[32,4096]{1,0:T(8,128)} copy(f32[32,4096]{0,1:T(8,128)} %broadcast_multiply_fusion) | data formatting | bytes 1048576
  266.3 11.0 %reduce-scatter.5.cloned.1.call-done = f32[128,512]{1,0:T(8,128)} async-done(((f32[256,512]{1,0:T(8,128)}), f32[128,512]{1,0:T(8,128)}) %reduce-scatter.5.cloned.1.call-update) | async-done | bytes 262160 | tf_op jit(solution)/shard_map/reduce_scatter | solution.py:85
  (96 shorter events, 43.3 us)
Async XLA Ops:
  7.2 6.7 %copy-start.1 = (bf16[128,6144]{1,0:T(8,128)(2,1)S(1)}, bf16[128,6144]{1,0:T(8,128)(2,1)}, u32[]{:S(2)}) copy-start(bf16[128,6144]{1,0:T(8,128)(2,1)} %param.15) | copy-start | bytes 4718596
  9.6 18.7 %all-to-all-start.1 = ((bf16[128,2,2048]{2,0,1:T(8,128)(2,1)}), bf16[128,2,2048]{2,0,1:T(8,128)(2,1)S(1)}, u32[]{:S(2)}, u32[]{:S(2)}) async-start(bf16[128,2,2048]{2,0,1:T(8,128)(2,1)} %bitcast.23), calls=%async_computation.1 | async-start | bytes 2097152 | tf_op jit(solution)/shard_map/all_to_all | solution.py:74
  15.1 16.9 %copy-start.3 = (bf16[128,64]{0,1:T(8,128)(2,1)S(1)}, bf16[128,64]{0,1:T(8,128)(2,1)}, u32[]{:S(2)}) copy-start(bf16[128,64]{0,1:T(8,128)(2,1)} %param.17) | copy-start | bytes 49156
  15.1 36.4 %copy-start.2 = (bf16[128,512]{1,0:T(8,128)(2,1)S(1)}, bf16[128,512]{1,0:T(8,128)(2,1)}, u32[]{:S(2)}) copy-start(bf16[128,512]{1,0:T(8,128)(2,1)} %param.16) | copy-start | bytes 393220
  28.3 33.7 %all-to-all-start = ((bf16[128,2,3072]{2,0,1:T(8,128)(2,1)}), bf16[128,2,3072]{2,0,1:T(8,128)(2,1)S(1)}, u32[]{:S(2)}, u32[]{:S(2)}) async-start(bf16[128,2,3072]{2,0,1:T(8,128)(2,1)} %bitcast.22), calls=%async_computation | async-start | bytes 3145728 | tf_op jit(solution)/shard_map/all_to_all | solution.py:73
  32.0 228.2 %reduce-scatter.7.cloned.1.call-start = ((), (), s32[]{:S(2)}) async-start(), calls=%async_computation.5 | async-start | bytes 8912896
  62.0 1.2 copy-start
  156.3 121.0 %reduce-scatter.5.cloned.1.call-start = ((), (), s32[]{:S(2)}) async-start(), calls=%async_computation.4 | async-start | bytes 786432 | tf_op jit(solution)/shard_map/reduce_scatter | solution.py:85
Sparse Core Ops, SparseCore 0:
  156.5 103.6 reduce-scatter.6
  263.0 14.2 reduce-scatter.4
where the time goes:
time: 287 us; the launch traced here: 284 us
  waiting for transfers between devices  124 us (43%)
  matrix products  90.6 us (32%)
  blocking collectives  25.1 us (9%)
  local copies, waits for them, and re-layouts  18.7 us (7%)
  between operations  14.1 us (5%)
  starting transfers between devices  8.02 us (3%)
  other arithmetic  2.94 us (1%)
    unnamed x3, waiting for transfers between devices  99.5 us
    all_gather x1, blocking collectives, per_device(): lax.all_gather(key_rope, 'seq', axis=0, tiled=True)  19.4 us
    dot_general x16, matrix products, head_block(): jnp.dot(score_grad.T, query_nope[row_start:row_end], preferred_element_ty...  19.2 us
    dot_general x16, matrix products, head_block(): jnp.dot(query_nope[row_start:row_end], keys_nope[:row_end].T, preferred_e...  18.7 us
    dot_general x16, matrix products, head_block(): jnp.dot(query_rope[row_start:row_end], rope_full[:row_end].T, preferred_e...  18.3 us
    dot_general x16, matrix products, head_block(): jnp.dot(grad_rows, values[:row_end].T, preferred_element_type=jnp.float32)  17.2 us
    unnamed x12, local copies, waits for them, and re-layouts  14.8 us
    all_to_all x1, waiting for transfers between devices, per_device(): lax.all_to_all(out_grad, 'seq', split_axis=1, concat_axis=0, tiled=True)  13.2 us
  transfers between devices with their start and end apart: 4, of which 3 were waited for; matrix products, arithmetic and copies ran while one was open for 6% of the time, Pallas kernels for 0%

commit v1 on v0

v1 whole, which is shorter than its diff:
```python
import functools
import math

import jax
import jax.numpy as jnp
from jax import lax
from jax.experimental import pallas as pl
from jax.experimental.pallas import tpu as pltpu
from jax.sharding import PartitionSpec as P

NOPE = 128
ROPE = 64
VDIM = 128
QW = NOPE + ROPE
KVW = NOPE + VDIM
PAIR_Q = 2 * QW
PAIR_G = 2 * VDIM
PAIR_KV = 2 * KVW
AHEAD = 4
MESH = pl.DeviceIdType.MESH
F32 = jnp.float32
BF16 = jnp.bfloat16
NT = (((1,), (1,)), ((), ()))


def kernel(
    n_seq, na, nb, pairs,
    q_hbm, lat_hbm, rope_hbm, w_hbm, g_hbm,
    lg_ref, wg_ref,
    qbuf, gbuf, wbuf, latbuf, ropebuf, lat_t, rope_l, rope_r, gc, lg_acc,
    part, dsend, drecv, keepx, xsend, xrecv, keepz, zsend, zrecv, lsend, lrecv,
    q_local, g_local, w_local, lat_local, rope_local,
    q_send, q_recv, g_send, g_recv, lat_send, lat_recv, rope_send, rope_recv,
    d_send, d_recv, x_send, x_recv, z_send, z_recv, l_send, l_recv,
):
    seq = lax.axis_index("seq")
    dp = lax.axis_index("dp")
    core = lax.rem(dp, 2)
    chip = dp // 2
    a_me = chip // nb
    b_me = lax.rem(chip, nb)
    n_chips = na * nb
    rows = lat_hbm.shape[0]
    length = n_seq * rows
    rank = lat_hbm.shape[1]
    block = rank // (2 * n_chips)
    scale = QW ** -0.5

    def seq_to(o):
        return lax.rem(seq + o, n_seq)

    def chip_core(a, b, c):
        return (a * nb + b) * 2 + c

    core_partner = chip_core(a_me, b_me, 1 - core)

    barrier = pltpu.get_barrier_semaphore()
    greeted = 0
    for o in range(1, n_seq):
        pl.semaphore_signal(barrier, inc=1, device_id={"seq": seq_to(o)}, device_id_type=MESH)
        greeted += 1
    pl.semaphore_signal(barrier, inc=1, device_id={"dp": core_partner}, device_id_type=MESH)
    greeted += 1
    for o in range(1, nb):
        pl.semaphore_signal(
            barrier, inc=1, device_id={"dp": chip_core(a_me, lax.rem(b_me + o, nb), core)},
            device_id_type=MESH,
        )
        greeted += 1
    for o in range(1, na):
        pl.semaphore_signal(
            barrier, inc=1, device_id={"dp": chip_core(lax.rem(a_me + o, na), b_me, core)},
            device_id_type=MESH,
        )
        greeted += 1

    def columns(owner, p, width):
        return pl.ds(pl.multiple_of((owner * pairs + p) * width, 128), width)

    def local_q(p):
        return pltpu.make_async_copy(
            q_hbm.at[:, columns(seq, p, PAIR_Q)], qbuf.at[p, seq], q_local.at[p]
        )

    def local_g(p):
        return pltpu.make_async_copy(
            g_hbm.at[:, columns(seq, p, PAIR_G)], gbuf.at[p, seq], g_local.at[p]
        )

    def local_w(p):
        return pltpu.make_async_copy(
            w_hbm.at[:, pl.ds(pl.multiple_of(p * PAIR_KV, 128), PAIR_KV)],
            wbuf.at[p], w_local.at[p],
        )

    local_lat = pltpu.make_async_copy(lat_hbm, latbuf.at[seq], lat_local)
    local_rope = pltpu.make_async_copy(rope_hbm, ropebuf.at[seq], rope_local)

    def remote(src, dst, send, recv, device):
        return pltpu.make_async_remote_copy(
            src_ref=src, dst_ref=dst, send_sem=send, recv_sem=recv,
            device_id=device, device_id_type=MESH,
        )

    def send_lat(o):
        return remote(lat_hbm, latbuf.at[seq], lat_send.at[o], lat_recv.at[o], {"seq": seq_to(o)})

    def send_rope(o):
        return remote(
            rope_hbm, ropebuf.at[seq], rope_send.at[o], rope_recv.at[o], {"seq": seq_to(o)}
        )

    def send_q(p, o):
        return remote(
            q_hbm.at[:, columns(seq_to(o), p, PAIR_Q)], qbuf.at[p, seq],
            q_send.at[p, o], q_recv.at[p, o], {"seq": seq_to(o)},
        )

    def send_g(p, o):
        return remote(
            g_hbm.at[:, columns(seq_to(o), p, PAIR_G)], gbuf.at[p, seq],
            g_send.at[p, o], g_recv.at[p, o], {"seq": seq_to(o)},
        )

    def send_d(p):
        return remote(dsend.at[p], drecv.at[p], d_send.at[p], d_recv.at[p], {"dp": core_partner})

    def send_x(p, o):
        return remote(
            xsend.at[p, o - 1], xrecv.at[p, o - 1], x_send.at[p, o - 1], x_recv.at[p, o - 1],
            {"dp": chip_core(a_me, lax.rem(b_me + o, nb), core)},
        )

    def send_z(p, o):
        return remote(
            zsend.at[p, o - 1], zrecv.at[p, o - 1], z_send.at[p, o - 1], z_recv.at[p, o - 1],
            {"dp": chip_core(lax.rem(a_me + o, na), b_me, core)},
        )

    def send_l(o):
        return remote(
            lsend.at[o - 1], lrecv.at[o - 1], l_send.at[o - 1], l_recv.at[o - 1],
            {"seq": seq_to(o)},
        )

    local_lat.start()
    local_rope.start()

    @pl.loop(0, pairs)
    def _(p):
        local_w(p).start()
        local_q(p).start()
        local_g(p).start()

    pl.semaphore_wait(barrier, greeted)

    for o in range(1, n_seq):
        send_lat(o).start()
        send_rope(o).start()

    def start_sends(p):
        for o in range(1, n_seq):
            send_q(p, o).start()
            send_g(p, o).start()

    @pl.loop(0, min(AHEAD, pairs))
    def _(p):
        start_sends(p)

    local_lat.wait()
    local_rope.wait()
    for o in range(1, n_seq):
        send_lat(o).wait_recv()
        send_rope(o).wait_recv()

    for s in range(n_seq):
        lat_t[:, s * rows:(s + 1) * rows] = latbuf[s].T
        rope = ropebuf[s]
        from_lane = lax.broadcasted_iota(jnp.int32, (ROPE, 128), 0)
        to_lane = lax.broadcasted_iota(jnp.int32, (ROPE, 128), 1)
        low = (from_lane == to_lane).astype(F32).astype(BF16)
        high = (from_lane + (128 - ROPE) == to_lane).astype(F32).astype(BF16)
        rope_l[s * rows:(s + 1) * rows] = jnp.dot(rope, low, preferred_element_type=F32)
        rope_r[s * rows:(s + 1) * rows] = jnp.dot(rope, high, preferred_element_type=F32)
    lg_acc[...] = jnp.zeros_like(lg_acc)

    span = math.gcd(length, 256)
    n_blocks = length // span
    lane = lax.broadcasted_iota(jnp.int32, (length, 128), 1)
    lower = lane < 64

    def head(keys, values, q_all, g_all):
        key_parts = [None] * n_blocks
        value_parts = [None] * n_blocks
        for b in range(n_blocks):
            end = (b + 1) * span
            q = q_all[b * span:end]
            g = g_all[b * span:end]
            scores = lax.dot_general(keys[:end], q, NT, preferred_element_type=F32) * scale
            key_pos = lax.broadcasted_iota(jnp.int32, (end, span), 0)
            query_pos = b * span + lax.broadcasted_iota(jnp.int32, (end, span), 1)
            scores = jnp.where(key_pos <= query_pos, scores, F32(-1e30))
            top = jnp.max(scores, axis=0, keepdims=True)
            expo = jnp.exp(scores - top)
            probs = expo * (1.0 / jnp.sum(expo, axis=0, keepdims=True))
            value_part = jnp.dot(probs.astype(BF16), g, preferred_element_type=F32)
            prob_grad = lax.dot_general(values[:end], g, NT, preferred_element_type=F32)
            row_dot = jnp.sum(probs * prob_grad, axis=0, keepdims=True)
            score_grad = (probs * (prob_grad - row_dot) * scale).astype(BF16)
            key_part = jnp.dot(score_grad, q, preferred_element_type=F32)
            for k in range(b + 1):
                at = slice(k * span, (k + 1) * span)
                if key_parts[k] is None:
                    key_parts[k], value_parts[k] = key_part[at], value_part[at]
                else:
                    key_parts[k] = key_parts[k] + key_part[at]
                    value_parts[k] = value_parts[k] + value_part[at]
        if n_blocks == 1:
            return key_parts[0], value_parts[0]
        return jnp.concatenate(key_parts, axis=0), jnp.concatenate(value_parts, axis=0)

    def compute(p):
        lat = latbuf[...].reshape(length, rank)
        local_w(p).wait()
        kv = jnp.dot(lat, wbuf[p], preferred_element_type=F32)
        keys0 = jnp.concatenate([kv[:, :128], rope_l[...]], axis=1).astype(BF16)
        turned = pltpu.roll(kv[:, 256:384], 64, 1)
        keys1 = jnp.concatenate(
            [jnp.where(lower, 0.0, turned), jnp.where(lower, turned, rope_r[...])], axis=1
        ).astype(BF16)
        local_q(p).wait()
        local_g(p).wait()
        for o in range(1, n_seq):
            send_q(p, o).wait_recv()
            send_g(p, o).wait_recv()
        q_all = qbuf[p].reshape(length, PAIR_Q)
        g_all = gbuf[p].reshape(length, PAIR_G)
        kg0, vg0 = head(keys0, kv[:, 128:256].astype(BF16), q_all[:, :256], g_all[:, :128])
        gc[:, 0:128] = kg0[:, :128].astype(BF16)
        gc[:, 128:256] = vg0.astype(BF16)
        kg1, vg1 = head(keys1, kv[:, 384:512].astype(BF16), q_all[:, 128:384], g_all[:, 128:])
        kg1 = jnp.where(lower, pltpu.roll(kg1[:, :128], 64, 1), pltpu.roll(kg1[:, 128:], 64, 1))
        gc[:, 256:384] = kg1.astype(BF16)
        gc[:, 384:512] = vg1.astype(BF16)
        grads = gc[...]
        slot = lax.rem(p, 2)
        product = jnp.dot(lat_t[...], grads, preferred_element_type=F32)
        for d in range(2 * n_chips):
            part[slot, d] = product[d * block:(d + 1) * block]
        for k in range(n_chips):
            dsend[p, k] = part[slot, 2 * k + 1 - core].astype(BF16)
        send_d(p).start()
        lg_acc[...] += lax.dot_general(grads, wbuf[p], NT, preferred_element_type=F32)

    def stage_x(p):
        slot = lax.rem(p, 2)
        send_d(p).wait_recv()

        def chip_sum(k):
            return part[slot, 2 * k + core] + drecv[p, k].astype(F32)

        for o in range(1, nb):
            b = lax.rem(b_me + o, nb)
            for a in range(na):
                xsend[p, o - 1, a] = chip_sum(a * nb + b).astype(BF16)
            send_x(p, o).start()
        for a in range(na):
            keepx[slot, a] = chip_sum(a * nb + b_me)

    def stage_z(p):
        slot = lax.rem(p, 2)
        for o in range(1, nb):
            send_x(p, o).wait_recv()

        def total(a):
            out = keepx[slot, a]
            for o in range(1, nb):
                out = out + xrecv[p, o - 1, a].astype(F32)
            return out

        for o in range(1, na):
            zsend[p, o - 1] = total(lax.rem(a_me + o, na)).astype(BF16)
            send_z(p, o).start()
        keepz[slot] = total(a_me)

    def stage_out(p):
        slot = lax.rem(p, 2)
        out = keepz[slot]
        for o in range(1, na):
            send_z(p, o).wait_recv()
            out = out + zrecv[p, o - 1].astype(F32)
        at = pl.ds(pl.multiple_of(p * PAIR_KV, 128), PAIR_KV)
        wg_ref[:, at] = out * (1.0 / (2 * n_chips))

    @pl.loop(0, pairs + 3)
    def _(step):
        @pl.when(step + AHEAD < pairs)
        def _():
            start_sends(step + AHEAD)

        @pl.when(step >= 3)
        def _():
            stage_out(step - 3)

        @pl.when((step >= 2) & (step < pairs + 2))
        def _():
            stage_z(step - 2)

        @pl.when((step >= 1) & (step < pairs + 1))
        def _():
            stage_x(step - 1)

        @pl.when(step < pairs)
        def _():
            compute(step)

        @pl.when(step == pairs - 1)
        def _():
            for o in range(1, n_seq):
                at = pl.ds(pl.multiple_of(seq_to(o) * rows, rows), rows)
                lsend[o - 1] = lg_acc[at, :]
                send_l(o).start()

    own = lg_acc[pl.ds(pl.multiple_of(seq * rows, rows), rows), :]
    for o in range(1, n_seq):
        send_l(o).wait_recv()
        own = own + lrecv[o - 1]
    lg_ref[...] = own

    for o in range(1, n_seq):
        send_lat(o).wait_send()
        send_rope(o).wait_send()
        send_l(o).wait_send()

    @pl.loop(0, pairs)
    def _(p):
        for o in range(1, n_seq):
            send_q(p, o).wait_send()
            send_g(p, o).wait_send()
        send_d(p).wait_send()
        for o in range(1, nb):
            send_x(p, o).wait_send()
        for o in range(1, na):
            send_z(p, o).wait_send()


def per_device(queries, latent, key_rope, up_weight, out_grad):
    n_seq = lax.axis_size("seq")
    n_dp = lax.axis_size("dp")
    n_chips = n_dp // 2
    na = math.gcd(n_chips, 4)
    nb = n_chips // na
    rows, rank = latent.shape
    length = n_seq * rows
    pairs = up_weight.shape[1] // PAIR_KV
    block = rank // n_dp
    width = PAIR_KV
    dma = pltpu.SemaphoreType.DMA
    xs, zs, ss = max(nb - 1, 1), max(na - 1, 1), max(n_seq - 1, 1)
    return pl.pallas_call(
        functools.partial(kernel, n_seq, na, nb, pairs),
        out_shape=(
            jax.ShapeDtypeStruct((rows, rank), F32),
            jax.ShapeDtypeStruct((block, pairs * width), F32),
        ),
        in_specs=[pl.BlockSpec(memory_space=pl.ANY)] * 5,
        out_specs=[pl.BlockSpec(memory_space=pltpu.VMEM)] * 2,
        scratch_shapes=[
            pltpu.VMEM((pairs, n_seq, rows, PAIR_Q), BF16),
            pltpu.VMEM((pairs, n_seq, rows, PAIR_G), BF16),
            pltpu.VMEM((pairs, rank, width), BF16),
            pltpu.VMEM((n_seq, rows, rank), BF16),
            pltpu.VMEM((n_seq, rows, ROPE), BF16),
            pltpu.VMEM((rank, length), BF16),
            pltpu.VMEM((length, 128), F32),
            pltpu.VMEM((length, 128), F32),
            pltpu.VMEM((length, width), BF16),
            pltpu.VMEM((length, rank), F32),
            pltpu.VMEM((2, n_dp, block, width), F32),
            pltpu.VMEM((pairs, n_chips, block, width), BF16),
            pltpu.VMEM((pairs, n_chips, block, width), BF16),
            pltpu.VMEM((2, na, block, width), F32),
            pltpu.VMEM((pairs, xs, na, block, width), BF16),
            pltpu.VMEM((pairs, xs, na, block, width), BF16),
            pltpu.VMEM((2, block, width), F32),
            pltpu.VMEM((pairs, zs, block, width), BF16),
            pltpu.VMEM((pairs, zs, block, width), BF16),
            pltpu.VMEM((ss, rows, rank), F32),
            pltpu.VMEM((ss, rows, rank), F32),
            dma((pairs,)), dma((pairs,)), dma((pairs,)), dma, dma,
            dma((pairs, n_seq)), dma((pairs, n_seq)), dma((pairs, n_seq)), dma((pairs, n_seq)),
            dma((n_seq,)), dma((n_seq,)), dma((n_seq,)), dma((n_seq,)),
            dma((pairs,)), dma((pairs,)),
            dma((pairs, xs)), dma((pairs, xs)), dma((pairs, zs)), dma((pairs, zs)),
            dma((ss,)), dma((ss,)),
        ],
        compiler_params=pltpu.CompilerParams(
            collective_id=0, has_side_effects=True, vmem_limit_bytes=60 * 1024 * 1024
        ),
    )(queries, latent, key_rope, up_weight, out_grad)


def solution(mesh):
    placed = (
        P(("dp", "seq"), None),
        P(("dp", "seq"), None),
        P(("dp", "seq"), None),
        P(None, "seq"),
        P(("dp", "seq"), None),
    )
    return jax.shard_map(
        per_device,
        mesh=mesh,
        in_specs=placed,
        out_specs=(P(("dp", "seq"), None), P("dp", "seq")),
        check_vma=False,
    )
```

time: 287 us -> 66.4 us (0.23)
  waiting for transfers between devices: 124 us -> 0 us
  matrix products: 90.6 us -> 0 us
  Pallas kernels: 0 us -> 60.6 us
  blocking collectives: 25.1 us -> 0 us
  local copies, waits for them, and re-layouts: 18.7 us -> 4.97 us
  between operations: 14.1 us -> 0.64 us
  starting transfers between devices: 8.02 us -> 0 us
  other arithmetic: 2.94 us -> 0 us
    unnamed x3 -> x0, waiting for transfers between devices: 99.5 us -> none
    dot_general x83 -> x0, matrix products: 90.6 us -> none  [the longest x16 19.2 us: head_block(): jnp.dot(score_grad.T, query_nope[row_start:row_end], preferred_element_ty...]
    pallas_call x0 -> x1, Pallas kernels: none -> 60.6 us  [per_device(): pl.pallas_call(functools.partial(kernel, n_seq, na, nb, pairs), out_shape...]
    all_gather x2 -> x0, blocking collectives: 25.1 us -> none  [the longest x1 19.4 us: per_device(): lax.all_gather(key_rope, 'seq', axis=0, tiled=True)]
    all_to_all x2 -> x0, waiting for transfers between devices: 13.2 us -> none  [the longest x1 13.2 us: per_device(): lax.all_to_all(out_grad, 'seq', split_axis=1, concat_axis=0, tiled=True)]
    reduce_scatter x1 -> x0, waiting for transfers between devices: 11 us -> none  [per_device(): lax.psum_scatter(latent_part, 'seq', scatter_dimension=0, tiled=True)]
    unnamed x12 -> x3, local copies, waits for them, and re-layouts: 14.8 us -> 4.97 us
    all_to_all x2 -> x0, starting transfers between devices: 7.93 us -> none  [the longest x1 4.26 us: per_device(): lax.all_to_all(out_grad, 'seq', split_axis=1, concat_axis=0, tiled=True)]
  transfers between devices with their start and end apart: 4 -> 0, of which waited for: 3 -> 0; matrix products, arithmetic and copies ran while one was open for 6% -> 0% of each run, Pallas kernels for 0% -> 0%
where the time goes in v1:
time: 66.4 us; the launch traced here: 66.2 us
  Pallas kernels  60.6 us (91%)
  local copies, waits for them, and re-layouts  4.97 us (7%)
    pallas_call x1, Pallas kernels, per_device(): pl.pallas_call(functools.partial(kernel, n_seq, na, nb, pairs), out_shape...  60.6 us
    unnamed x3, local copies, waits for them, and re-layouts  4.97 us

profile of v1, /device:TPU:0, one launch (start us, length us, event | category | flops | bytes accessed | tf_op | source)
XLA Modules:
  0.0 66.2 jit_solution(2341337469692131137)
XLA Ops:
  0.6 1.4 %copy.7.rope_hbm = bf16[128,64]{1,0:T(8,128)(2,1)} copy(bf16[128,64]{0,1:T(8,128)(2,1)} %param.7) | data formatting | bytes 32768 | tf_op args[2]
  2.1 60.6 %shard_map.68 = (f32[128,512]{1,0:T(8,128)}, f32[32,4096]{1,0:T(8,128)}) custom-call(bf16[128,6144]{1,0:T(8,128)(2,1)} %q_hbm.1, bf16[128,512]{1,0:T(8,128)(2,1)} %lat_hbm.1, bf16[128,64]{1,0:T(8,128)(2,1)} %copy.7.rope_hbm, bf16[512,4096]{1,0:T(8,128)(2,1)} %w_hbm.1, bf16[128,4096]{1,0:T(8,128)(2,1)} %g_hbm.1), custom_call_target="tpu_custom_call" | custom-call | tf_op jit(solution)/shard_map/pallas_call | solution.py:360
  62.6 1.7 %copy.10 = f32[128,512]{1,0:T(8,128)} copy(f32[128,512]{1,0:T(8,128)} %get-tuple-element.4) | data formatting | bytes 524288
  64.3 1.9 %copy.11 = f32[32,4096]{1,0:T(8,128)} copy(f32[32,4096]{1,0:T(8,128)} %get-tuple-element.5) | data formatting | bytes 1048576

commit v2 on v1

--- a/solution.py
+++ b/solution.py
@@ -17,17 +17,19 @@
 PAIR_G = 2 * VDIM
 PAIR_KV = 2 * KVW
 AHEAD = 4
+Z_LAG = 3
 MESH = pl.DeviceIdType.MESH
 F32 = jnp.float32
 BF16 = jnp.bfloat16
 NT = (((1,), (1,)), ((), ()))
+TN = (((0,), (0,)), ((), ()))
 
 
 def kernel(
     n_seq, na, nb, pairs,
     q_hbm, lat_hbm, rope_hbm, w_hbm, g_hbm,
     lg_ref, wg_ref,
-    qbuf, gbuf, wbuf, latbuf, ropebuf, lat_t, rope_l, rope_r, gc, lg_acc,
+    qbuf, gbuf, wbuf, latbuf, ropebuf, lat_t, rope_l, rope_r, keys, values, gc, lg_acc,
     part, dsend, drecv, keepx, xsend, xrecv, keepz, zsend, zrecv, lsend, lrecv,
     q_local, g_local, w_local, lat_local, rope_local,
     q_send, q_recv, g_send, g_recv, lat_send, lat_recv, rope_send, rope_recv,
@@ -180,8 +182,8 @@
         to_lane = lax.broadcasted_iota(jnp.int32, (ROPE, 128), 1)
         low = (from_lane == to_lane).astype(F32).astype(BF16)
         high = (from_lane + (128 - ROPE) == to_lane).astype(F32).astype(BF16)
-        rope_l[s * rows:(s + 1) * rows] = jnp.dot(rope, low, preferred_element_type=F32)
-        rope_r[s * rows:(s + 1) * rows] = jnp.dot(rope, high, preferred_element_type=F32)
+        rope_l[s * rows:(s + 1) * rows] = lax.dot_general(rope, low, TN, preferred_element_type=F32)
+        rope_r[s * rows:(s + 1) * rows] = lax.dot_general(rope, high, TN, preferred_element_type=F32)
     lg_acc[...] = jnp.zeros_like(lg_acc)
 
     span = math.gcd(length, 256)
@@ -189,14 +191,14 @@
     lane = lax.broadcasted_iota(jnp.int32, (length, 128), 1)
     lower = lane < 64
 
-    def head(keys, values, q_all, g_all):
+    def head(head_keys, head_values, q_all, g_all):
         key_parts = [None] * n_blocks
         value_parts = [None] * n_blocks
         for b in range(n_blocks):
             end = (b + 1) * span
             q = q_all[b * span:end]
             g = g_all[b * span:end]
-            scores = lax.dot_general(keys[:end], q, NT, preferred_element_type=F32) * scale
+            scores = lax.dot_general(head_keys[:end], q, NT, preferred_element_type=F32) * scale
             key_pos = lax.broadcasted_iota(jnp.int32, (end, span), 0)
             query_pos = b * span + lax.broadcasted_iota(jnp.int32, (end, span), 1)
             scores = jnp.where(key_pos <= query_pos, scores, F32(-1e30))
@@ -204,7 +206,7 @@
             expo = jnp.exp(scores - top)
             probs = expo * (1.0 / jnp.sum(expo, axis=0, keepdims=True))
             value_part = jnp.dot(probs.astype(BF16), g, preferred_element_type=F32)
-            prob_grad = lax.dot_general(values[:end], g, NT, preferred_element_type=F32)
+            prob_grad = lax.dot_general(head_values[:end], g, NT, preferred_element_type=F32)
             row_dot = jnp.sum(probs * prob_grad, axis=0, keepdims=True)
             score_grad = (probs * (prob_grad - row_dot) * scale).astype(BF16)
             key_part = jnp.dot(score_grad, q, preferred_element_type=F32)
@@ -219,15 +221,19 @@
             return key_parts[0], value_parts[0]
         return jnp.concatenate(key_parts, axis=0), jnp.concatenate(value_parts, axis=0)
 
-    def compute(p):
+    def make_keys(p):
         lat = latbuf[...].reshape(length, rank)
         local_w(p).wait()
         kv = jnp.dot(lat, wbuf[p], preferred_element_type=F32)
-        keys0 = jnp.concatenate([kv[:, :128], rope_l[...]], axis=1).astype(BF16)
+        keys[0] = jnp.concatenate([kv[:, :128], rope_l[...]], axis=1).astype(BF16)
         turned = pltpu.roll(kv[:, 256:384], 64, 1)
-        keys1 = jnp.concatenate(
+        keys[1] = jnp.concatenate(
             [jnp.where(lower, 0.0, turned), jnp.where(lower, turned, rope_r[...])], axis=1
         ).astype(BF16)
+        values[0] = kv[:, 128:256].astype(BF16)
+        values[1] = kv[:, 384:512].astype(BF16)
+
+    def compute(p):
         local_q(p).wait()
         local_g(p).wait()
         for o in range(1, n_seq):
@@ -235,10 +241,10 @@
             send_g(p, o).wait_recv()
         q_all = qbuf[p].reshape(length, PAIR_Q)
         g_all = gbuf[p].reshape(length, PAIR_G)
-        kg0, vg0 = head(keys0, kv[:, 128:256].astype(BF16), q_all[:, :256], g_all[:, :128])
+        kg0, vg0 = head(keys[0], values[0], q_all[:, :256], g_all[:, :128])
         gc[:, 0:128] = kg0[:, :128].astype(BF16)
         gc[:, 128:256] = vg0.astype(BF16)
-        kg1, vg1 = head(keys1, kv[:, 384:512].astype(BF16), q_all[:, 128:384], g_all[:, 128:])
+        kg1, vg1 = head(keys[1], values[1], q_all[:, 128:384], g_all[:, 128:])
         kg1 = jnp.where(lower, pltpu.roll(kg1[:, :128], 64, 1), pltpu.roll(kg1[:, 128:], 64, 1))
         gc[:, 256:384] = kg1.astype(BF16)
         gc[:, 384:512] = vg1.astype(BF16)
@@ -265,15 +271,14 @@
                 xsend[p, o - 1, a] = chip_sum(a * nb + b).astype(BF16)
             send_x(p, o).start()
         for a in range(na):
-            keepx[slot, a] = chip_sum(a * nb + b_me)
+            keepx[p, a] = chip_sum(a * nb + b_me)
 
     def stage_z(p):
-        slot = lax.rem(p, 2)
         for o in range(1, nb):
             send_x(p, o).wait_recv()
 
         def total(a):
-            out = keepx[slot, a]
+            out = keepx[p, a]
             for o in range(1, nb):
                 out = out + xrecv[p, o - 1, a].astype(F32)
             return out
@@ -281,34 +286,33 @@
         for o in range(1, na):
             zsend[p, o - 1] = total(lax.rem(a_me + o, na)).astype(BF16)
             send_z(p, o).start()
-        keepz[slot] = total(a_me)
+        keepz[p] = total(a_me)
 
     def stage_out(p):
-        slot = lax.rem(p, 2)
-        out = keepz[slot]
+        out = keepz[p]
         for o in range(1, na):
             send_z(p, o).wait_recv()
             out = out + zrecv[p, o - 1].astype(F32)
         at = pl.ds(pl.multiple_of(p * PAIR_KV, 128), PAIR_KV)
         wg_ref[:, at] = out * (1.0 / (2 * n_chips))
 
-    @pl.loop(0, pairs + 3)
+    @pl.loop(0, pairs + Z_LAG)
     def _(step):
         @pl.when(step + AHEAD < pairs)
         def _():
             start_sends(step + AHEAD)
 
-        @pl.when(step >= 3)
-        def _():
-            stage_out(step - 3)
-
-        @pl.when((step >= 2) & (step < pairs + 2))
-        def _():
-            stage_z(step - 2)
+        @pl.when(step < pairs)
+        def _():
+            make_keys(step)
 
         @pl.when((step >= 1) & (step < pairs + 1))
         def _():
             stage_x(step - 1)
+
+        @pl.when(step >= Z_LAG)
+        def _():
+            stage_z(step - Z_LAG)
 
         @pl.when(step < pairs)
         def _():
@@ -326,6 +330,10 @@
         send_l(o).wait_recv()
         own = own + lrecv[o - 1]
     lg_ref[...] = own
+
+    @pl.loop(0, pairs)
+    def _(p):
+        stage_out(p)
 
     for o in range(1, n_seq):
         send_lat(o).wait_send()
@@ -357,7 +365,7 @@
     width = PAIR_KV
     dma = pltpu.SemaphoreType.DMA
     xs, zs, ss = max(nb - 1, 1), max(na - 1, 1), max(n_seq - 1, 1)
-    return pl.pallas_call(
+    results = pl.pallas_call(
         functools.partial(kernel, n_seq, na, nb, pairs),
         out_shape=(
             jax.ShapeDtypeStruct((rows, rank), F32),
@@ -370,19 +378,21 @@
             pltpu.VMEM((pairs, n_seq, rows, PAIR_G), BF16),
             pltpu.VMEM((pairs, rank, width), BF16),
             pltpu.VMEM((n_seq, rows, rank), BF16),
-            pltpu.VMEM((n_seq, rows, ROPE), BF16),
+            pltpu.VMEM((n_seq, ROPE, rows), BF16),
             pltpu.VMEM((rank, length), BF16),
             pltpu.VMEM((length, 128), F32),
             pltpu.VMEM((length, 128), F32),
+            pltpu.VMEM((2, length, 256), BF16),
+            pltpu.VMEM((2, length, 128), BF16),
             pltpu.VMEM((length, width), BF16),
             pltpu.VMEM((length, rank), F32),
             pltpu.VMEM((2, n_dp, block, width), F32),
             pltpu.VMEM((pairs, n_chips, block, width), BF16),
             pltpu.VMEM((pairs, n_chips, block, width), BF16),
-            pltpu.VMEM((2, na, block, width), F32),
+            pltpu.VMEM((pairs, na, block, width), F32),
             pltpu.VMEM((pairs, xs, na, block, width), BF16),
             pltpu.VMEM((pairs, xs, na, block, width), BF16),
-            pltpu.VMEM((2, block, width), F32),
+            pltpu.VMEM((pairs, block, width), F32),
             pltpu.VMEM((pairs, zs, block, width), BF16),
             pltpu.VMEM((pairs, zs, block, width), BF16),
             pltpu.VMEM((ss, rows, rank), F32),
@@ -397,7 +407,25 @@
         compiler_params=pltpu.CompilerParams(
             collective_id=0, has_side_effects=True, vmem_limit_bytes=60 * 1024 * 1024
         ),
-    )(queries, latent, key_rope, up_weight, out_grad)
+    )(queries, latent, key_rope.T, up_weight, out_grad)
+    return pl.pallas_call(
+        put_out,
+        out_shape=tuple(jax.ShapeDtypeStruct(r.shape, r.dtype) for r in results),
+        in_specs=[pl.BlockSpec(memory_space=pltpu.VMEM)] * 2,
+        out_specs=[pl.BlockSpec(memory_space=pl.ANY)] * 2,
+        scratch_shapes=[pltpu.SemaphoreType.DMA((2,))],
+    )(*results)
+
+
+def put_out(lg_in, wg_in, lg_out, wg_out, sems):
+    copies = (
+        pltpu.make_async_copy(lg_in, lg_out, sems.at[0]),
+        pltpu.make_async_copy(wg_in, wg_out, sems.at[1]),
+    )
+    for copy in copies:
+        copy.start()
+    for copy in copies:
+        copy.wait()
 
 
 def solution(mesh):

time: 66.4 us -> 56.8 us (0.86)
  local copies, waits for them, and re-layouts: 4.97 us -> 0 us
  Pallas kernels: 60.6 us -> 56 us
    pallas_call x1, Pallas kernels: 60.6 us -> 54 us  [per_device(): pl.pallas_call(functools.partial(kernel, n_seq, na, nb, pairs), out_shape...]
    unnamed x3 -> x0, local copies, waits for them, and re-layouts: 4.97 us -> none
    pallas_call x0 -> x1, Pallas kernels: none -> 2.02 us  [per_device(): pl.pallas_call(put_out, out_shape=tuple((jax.ShapeDtypeStruct(r.shape, r....]
where the time goes in v2:
time: 56.8 us; the launch traced here: 56.6 us
  Pallas kernels  56 us (99%)
  between operations  0.64 us (1%)
    pallas_call x1, Pallas kernels, per_device(): pl.pallas_call(functools.partial(kernel, n_seq, na, nb, pairs), out_shape...  54 us
    pallas_call x1, Pallas kernels, per_device(): pl.pallas_call(put_out, out_shape=tuple((jax.ShapeDtypeStruct(r.shape, r....  2.02 us

profile of v2, /device:TPU:0, one launch (start us, length us, event | category | flops | bytes accessed | tf_op | source)
XLA Modules:
  0.0 56.6 jit_solution(2356127234384499851)
XLA Ops:
  0.6 54.0 %shard_map.68 = (f32[128,512]{1,0:T(8,128)}, f32[32,4096]{1,0:T(8,128)}) custom-call(bf16[128,6144]{1,0:T(8,128)(2,1)} %q_hbm.1, bf16[128,512]{1,0:T(8,128)(2,1)} %lat_hbm.1, bf16[64,128]{1,0:T(8,128)(2,1)} %bitcast.1, bf16[512,4096]{1,0:T(8,128)(2,1)} %w_hbm.1, bf16[128,4096]{1,0:T(8,128)(2,1)} %g_hbm.1), custom_call_target="tpu_custom_call" | custom-call | tf_op jit(solution)/shard_map/pallas_call | solution.py:368
  54.6 2.0 %shard_map.69 = (f32[128,512]{1,0:T(8,128)}, f32[32,4096]{1,0:T(8,128)}) custom-call(f32[128,512]{1,0:T(8,128)} %get-tuple-element.4.lg_in, f32[32,4096]{1,0:T(8,128)} %get-tuple-element.5.wg_in), custom_call_target="tpu_custom_call" | custom-call | tf_op jit(solution)/shard_map/pallas_call | solution.py:411
